TPU v7x, 32 devices: a whole 2x2x4 slice. The times are simulated.
32 devices in a mesh: row: 8 (over z, core), col: 4 (over y, x).
Axes of the slice: x: 2, y: 2, z: 4, core: 2. Of those that a mesh axis runs over, the one named last changes fastest.
Arguments:
- pair_exchange: bfloat16 [64, 16, 1024], P(('row', 'col')), may hold values from -6 to 6
- conduction: bfloat16 [64, 4, 1024], P(('row', 'col')), may hold values from -6 to 6
- valence: bfloat16 [64, 4, 1024], P(('row', 'col')), may hold values from -6 to 6
- coulomb: float32 [1024], replicated, may hold values from 0.5 to 5
- screening: float32 [34, 1024], replicated, may hold values from 0.1 to 1
- energies: float32 [64, 16], P(('row', 'col')), may hold values from 1 to 9
- vectors: bfloat16 [64, 512], P(('row', 'col')), may hold values from -6 to 6
- k_coords: int32 [64, 2], P(('row', 'col')), may hold values from 0 to 31, as said below
Outputs:
- residual_block: float32 [64, 512], P(('row', 'col'))
- alpha: float32 [32, 32], replicated
Inputs may be any that keep to these rules, and one draw needn't show every extreme that they name: `k_coords`: each row holds a k-point's coordinates on the periodic 32 x 2 mesh, first then second; every mesh point occurs exactly once.
All inputs are finite; a program needn't handle non-finite values.
Results may differ from a plain program's by a relative error of at most 0.0028.
Values may be sent and summed in bfloat16 or wider, within the bound.
A program may use at most 64 MiB of HBM per device.

v0:
```python
import jax
import jax.numpy as jnp
from jax import lax
from jax.sharding import PartitionSpec as P

MX = 32
highest = lax.Precision.HIGHEST


def pair_factors(conduction, valence):
    count, valence_count, plane_count = valence.shape
    joined = (
        valence.astype(jnp.float32)[:, :, None, :] * conduction.astype(jnp.float32)[:, None, :, :]
    )
    return joined.reshape(count, valence_count * conduction.shape[1], plane_count).astype(
        jnp.bfloat16
    )


def transfer_index(rows_at, cols_at, mesh_cols):
    delta_first = jnp.mod(rows_at[:, None, 0] - cols_at[None, :, 0], MX)
    delta_second = jnp.mod(rows_at[:, None, 1] - cols_at[None, :, 1], mesh_cols)
    fold_first = jnp.minimum(delta_first, MX - delta_first)
    fold_second = jnp.minimum(delta_second, mesh_cols - delta_second)
    return (fold_first * (mesh_cols // 2 + 1) + fold_second).astype(jnp.int32)


def on_device(pair_exchange, conduction, valence, coulomb, screening, energies, vectors, k_coords):
    local_count, band_count, plane_count = pair_exchange.shape
    vector_count = vectors.shape[1] // band_count
    row_count = lax.axis_size("row")
    col_count = lax.axis_size("col")
    total_count = local_count * row_count * col_count
    mesh_cols = total_count // MX
    moving = vectors.reshape(local_count, band_count, vector_count)
    partial_density = jnp.einsum(
        "ktg,ktn->gn", pair_exchange, moving, preferred_element_type=jnp.float32
    )
    density = lax.psum(partial_density, ("row", "col"))
    block_size = 128
    sweeps = plane_count // block_size
    col_cond, col_val, col_vec, col_at = (
        lax.all_gather(conduction, "row", axis=0, tiled=True),
        lax.all_gather(valence, "row", axis=0, tiled=True),
        lax.all_gather(vectors, "row", axis=0, tiled=True),
        lax.all_gather(k_coords, "row", axis=0, tiled=True),
    )
    row_cond, row_val, row_at = (
        lax.all_gather(conduction, "col", axis=0, tiled=True),
        lax.all_gather(valence, "col", axis=0, tiled=True),
        lax.all_gather(k_coords, "col", axis=0, tiled=True),
    )
    row_pairs = pair_factors(row_cond, row_val)
    col_pairs = pair_factors(col_cond, col_val)
    indices = transfer_index(row_at, col_at, mesh_cols)
    col_moving = col_vec.reshape(-1, band_count, vector_count)

    def square_sweep(sweep_index, running):
        anchor = sweep_index * block_size
        coupling = jnp.take(
            lax.dynamic_slice_in_dim(screening, anchor, block_size, 1), indices, axis=0
        )
        row_block = lax.dynamic_slice_in_dim(row_pairs, anchor, block_size, 2)
        col_block = lax.dynamic_slice_in_dim(col_pairs, anchor, block_size, 2)
        col_proj = jnp.einsum(
            "ktg,ktn->kng", col_block, col_moving, preferred_element_type=jnp.float32
        )
        potential = jnp.einsum("ijg,jng->ing", coupling, col_proj, precision=highest)
        return running + jnp.einsum(
            "ktg,kng->ktn", row_block.astype(jnp.float32), potential, precision=highest
        )

    forward = lax.fori_loop(
        0,
        sweeps,
        square_sweep,
        jnp.zeros((row_pairs.shape[0], band_count, vector_count), jnp.float32),
    )
    owned = lax.psum_scatter(
        forward.reshape(col_count, local_count, band_count, vector_count),
        "col",
        scatter_dimension=0,
        tiled=True,
    )[0]
    moving_wide = moving.astype(jnp.float32)
    exchange_term = jnp.einsum(
        "ktg,gn->ktn", pair_exchange.astype(jnp.float32) * coulomb, density, precision=highest
    )
    applied = (
        energies[:, :, None] * moving_wide
        + 2.0 / (total_count * band_count) * exchange_term
        - owned / total_count
    )
    gram = jnp.einsum("ktm,ktn->mn", moving_wide, applied, precision=highest)
    alpha = lax.psum(gram, ("row", "col")) / (total_count * band_count)
    residual = applied - jnp.einsum("ktm,mn->ktn", moving_wide, alpha, precision=highest)
    return (residual.reshape(local_count, band_count * vector_count), alpha)


def solution(mesh):
    in_specs = (
        P(("row", "col"), None, None),
        P(("row", "col"), None, None),
        P(("row", "col"), None, None),
        P(),
        P(),
        P(("row", "col"), None),
        P(("row", "col"), None),
        P(("row", "col"), None),
    )
    out_specs = (P(("row", "col"), None), P())
    return jax.shard_map(
        on_device, mesh=mesh, in_specs=in_specs, out_specs=out_specs, check_vma=False
    )
```

profile of v0, /device:TPU:0, one launch (start us, length us, event | category | flops | bytes accessed | tf_op | source)
XLA Modules:
  0.0 299.9 jit_solution(13418184121838847277)
XLA Ops:
  8.7 13.5 %all-gather.2 = s32[8,2,2]{2,1,0:T(2,128)S(1)} all-gather(s32[1,2,2]{2,1,0:T(2,128)S(1)} %bitcast.65), channel_id=1, replica_groups=mesh['row'=8,'col'=4] {'row'}, dimensions={0}, use_global_device_ids=true | all-gather | bytes 144 | tf_op jit(solution)/shard_map/all_gather | solution.py:46
  22.1 8.1 %all-gather.1 = s32[4,2,2]{2,1,0:T(2,128)S(1)} all-gather(s32[1,2,2]{2,1,0:T(2,128)S(1)} %bitcast.66), channel_id=1, replica_groups=mesh['row'=8,'col'=4] {'col'}, dimensions={0}, use_global_device_ids=true | all-gather | bytes 80 | tf_op jit(solution)/shard_map/all_gather | solution.py:51
  30.2 14.3 %all_gather.23 = bf16[16,4,1024]{2,1,0:T(4,128)(2,1)S(1)} all-gather(bf16[2,4,1024]{2,1,0:T(4,128)(2,1)} %param.12), channel_id=1, replica_groups=mesh['row'=8,'col'=4] {'row'}, dimensions={0}, use_global_device_ids=true | all-gather | bytes 147456 | tf_op jit(solution)/shard_map/all_gather | solution.py:44
  44.5 8.3 %all_gather.21 = bf16[8,4,1024]{2,1,0:T(4,128)(2,1)S(1)} all-gather(bf16[2,4,1024]{2,1,0:T(4,128)(2,1)S(1)} %copy-done.2), channel_id=1, replica_groups=mesh['row'=8,'col'=4] {'col'}, dimensions={0}, use_global_device_ids=true | all-gather | bytes 81920 | tf_op jit(solution)/shard_map/all_gather | solution.py:50
  52.9 14.0 %all_gather.24 = bf16[16,4,1024]{2,1,0:T(4,128)(2,1)S(1)} all-gather(bf16[2,4,1024]{2,1,0:T(4,128)(2,1)S(1)} %copy-done.3), channel_id=1, replica_groups=mesh['row'=8,'col'=4] {'row'}, dimensions={0}, use_global_device_ids=true | all-gather | bytes 147456 | tf_op jit(solution)/shard_map/all_gather | solution.py:43
  66.9 7.2 %all_gather.22 = bf16[8,4,1024]{2,1,0:T(4,128)(2,1)S(1)} all-gather(bf16[2,4,1024]{2,1,0:T(4,128)(2,1)S(1)} %copy-done.3), channel_id=1, replica_groups=mesh['row'=8,'col'=4] {'col'}, dimensions={0}, use_global_device_ids=true | all-gather | bytes 81920 | tf_op jit(solution)/shard_map/all_gather | solution.py:49
  75.8 12.8 %all-gather = bf16[8,2,512]{2,1,0:T(2,128)(2,1)S(1)} all-gather(bf16[1,2,512]{2,1,0:T(2,128)(2,1)S(1)} %bitcast.64), channel_id=1, replica_groups=mesh['row'=8,'col'=4] {'row'}, dimensions={0}, use_global_device_ids=true | all-gather | bytes 18432 | tf_op jit(solution)/shard_map/all_gather | solution.py:45
  88.7 33.2 %while.14 = (s32[]{:T(128)}, f32[8,16,32]{2,1,0:T(8,128)S(1)}, bf16[8,16,1024]{2,1,0:T(8,128)(2,1)S(1)}, bf16[16,16,1024]{2,1,0:T(8,128)(2,1)S(1)}, bf16[16,16,3...) while((s32[]{:T(128)}, f32[8,16,32]{2,1,0:T(8,128)S(1)}, ...), condition=%wide.region_2.3_spmd.clone, body=%wide.region_1.2_spmd.clone.sunk | while | flops 14714503 | bytes 2319689 | solution.py:73
  88.7 0.7 constant_dynamic-slice_fusion.2
  89.6 0.6 gather_fusion
  91.4 1.1 convolution_bitcast_fusion.8
  92.9 0.7 constant_dynamic-slice_fusion.2
  95.5 1.1 convolution_bitcast_fusion.8
  97.0 0.7 constant_dynamic-slice_fusion.2
  99.7 1.1 convolution_bitcast_fusion.8
  101.2 0.7 constant_dynamic-slice_fusion.2
  103.8 1.1 convolution_bitcast_fusion.8
  105.3 0.7 constant_dynamic-slice_fusion.2
  108.0 1.1 convolution_bitcast_fusion.8
  109.5 0.7 constant_dynamic-slice_fusion.2
  112.1 1.1 convolution_bitcast_fusion.8
  113.6 0.7 constant_dynamic-slice_fusion.2
  116.3 1.1 convolution_bitcast_fusion.8
  117.8 0.7 constant_dynamic-slice_fusion.2
  120.4 1.1 convolution_bitcast_fusion.8
  122.8 0.9 convolution_bitcast_fusion.2
  123.7 20.8 %reduce-scatter.4.cloned.1.call-done = f32[1,2,16,32]{3,2,1,0:T(8,128)} async-done(((f32[4,2,16,32]{3,2,1,0:T(8,128)}), f32[1,2,16,32]{3,2,1,0:T(8,128)}) %reduce-scatter.4.cloned.1.call-update) | async-done | bytes 4112
  144.5 105.8 %all-reduce.3.cloned.1.call-done = f32[1024,32]{0,1:T(8,128)} async-done(((f32[1024,32]{0,1:T(8,128)}), f32[1024,32]{0,1:T(8,128)}) %all-reduce.3.cloned.1.call-update) | async-done | bytes 131088 | tf_op jit(solution)/shard_map/psum | solution.py:39
  250.3 1.1 fusion.17
  251.7 39.3 %psum.15 = f32[32,32]{0,1:T(8,128)S(1)} all-reduce(f32[32,32]{0,1:T(8,128)S(1)} %convolution_bitcast_fusion.4), channel_id=1, replica_groups=mesh['row'=8,'col'=4] {'row','col'}, use_global_device_ids=true, to_apply=%region_4.5 | all-reduce | flops 1024 | bytes 8192 | tf_op jit(solution)/shard_map/psum | solution.py:95
  291.1 0.7 reshape.61
  291.8 0.7 copy.24
  (111 shorter events, 21.2 us)
Async XLA Ops:
  8.0 0.7 copy-start.6
  8.0 136.5 %reduce-scatter.4.cloned.1.call-start = ((), (), s32[]{:S(2)}) async-start(), calls=%async_computation.2 | async-start | bytes 81920
  30.2 14.3 %copy-start.2 = (bf16[2,4,1024]{2,1,0:T(4,128)(2,1)S(1)}, bf16[2,4,1024]{2,1,0:T(4,128)(2,1)}, u32[]{:S(2)}) copy-start(bf16[2,4,1024]{2,1,0:T(4,128)(2,1)} %param.12) | copy-start | bytes 49156
  44.5 8.3 %copy-start.3 = (bf16[2,4,1024]{2,1,0:T(4,128)(2,1)S(1)}, bf16[2,4,1024]{2,1,0:T(4,128)(2,1)}, u32[]{:S(2)}) copy-start(bf16[2,4,1024]{2,1,0:T(4,128)(2,1)} %param.11) | copy-start | bytes 49156
  75.2 0.7 copy-start.4
  121.9 0.6 copy-start
  121.9 0.9 copy-start.1
  122.6 127.7 %all-reduce.3.cloned.1.call-start = ((), (), s32[]{:S(2)}) async-start(), calls=%async_computation.1 | async-start | bytes 262144 | tf_op jit(solution)/shard_map/psum | solution.py:39
  123.7 126.6 %copy-start.5 = (f32[1024]{0:T(1024)S(1)}, f32[1024]{0:T(1024)}, u32[]{:S(2)}) copy-start(f32[1024]{0:T(1024)} %param.13) | copy-start | bytes 12292
  123.7 126.7 %copy-start.7 = (f32[2,16]{1,0:T(2,128)S(1)}, f32[2,16]{1,0:T(2,128)}, u32[]{:S(2)}) copy-start(f32[2,16]{1,0:T(2,128)} %param.15) | copy-start | bytes 388
Sparse Core Ops, SparseCore 0:
  122.7 21.7 reduce-scatter.3
Sparse Core Ops, SparseCore 1:
  128.6 121.7 all-reduce.2
where the time goes:
time: 301 us; the launch traced here: 300 us
  waiting for transfers between devices  127 us (42%)
  blocking collectives  117 us (39%)
  local copies, waits for them, and re-layouts  21.7 us (7%)
  matrix products  16.1 us (5%)
  between operations  15.6 us (5%)
    psum x1, waiting for transfers between devices, on_device(): density = lax.psum(partial_density, ('row', 'col'))  106 us
    psum x1, blocking collectives, on_device(): alpha = lax.psum(gram, ('row', 'col')) / (total_count * band_count)  39.3 us
    unnamed x3, waiting for transfers between devices  20.8 us
    all_gather x1, blocking collectives, on_device(): lax.all_gather(valence, 'row', axis=0, tiled=True)  14.3 us
    all_gather x1, blocking collectives, on_device(): lax.all_gather(conduction, 'row', axis=0, tiled=True)  14 us
    all_gather x1, blocking collectives, on_device(): lax.all_gather(k_coords, 'row', axis=0, tiled=True)  13.5 us
    all_gather x1, blocking collectives, on_device(): lax.all_gather(vectors, 'row', axis=0, tiled=True)  12.8 us
    dot_general x8, matrix products, square_sweep(): jnp.einsum('ijg,jng->ing', coupling, col_proj, precision=highest)  8.7 us
  transfers between devices with their start and end apart: 2, of which 2 were waited for; matrix products, arithmetic and copies ran while one was open for 0% of the time, Pallas kernels for 0%

commit v1 on v0

--- a/solution.py
+++ b/solution.py
@@ -36,7 +36,7 @@
     partial_density = jnp.einsum(
         "ktg,ktn->gn", pair_exchange, moving, preferred_element_type=jnp.float32
     )
-    density = lax.psum(partial_density, ("row", "col"))
+    density = lax.psum(lax.psum(partial_density, "row"), "col")
     block_size = 128
     sweeps = plane_count // block_size
     col_cond, col_val, col_vec, col_at = (

time: 301 us -> 242 us (0.80)
  waiting for transfers between devices: 127 us -> 66.3 us
    psum x1 -> x2, waiting for transfers between devices: 106 us -> 44.5 us  [on_device(): density = lax.psum(lax.psum(partial_density, 'row'), 'col')]
    unnamed x3 -> x4, waiting for transfers between devices: 20.8 us -> 21.7 us
  transfers between devices with their start and end apart: 2 -> 3, of which waited for: 2 -> 2; matrix products, arithmetic and copies ran while one was open for 0% -> 14% of each run, Pallas kernels for 0% -> 0%
where the time goes in v1:
time: 242 us; the launch traced here: 241 us
  blocking collectives  117 us (48%)
  waiting for transfers between devices  66.3 us (27%)
  local copies, waits for them, and re-layouts  22.3 us (9%)
  matrix products  17 us (7%)
  between operations  15.6 us (6%)
    psum x2, waiting for transfers between devices, on_device(): density = lax.psum(lax.psum(partial_density, 'row'), 'col')  44.5 us
    psum x1, blocking collectives, on_device(): alpha = lax.psum(gram, ('row', 'col')) / (total_count * band_count)  39.3 us
    unnamed x4, waiting for transfers between devices  21.7 us
    all_gather x1, blocking collectives, on_device(): lax.all_gather(conduction, 'row', axis=0, tiled=True)  14 us
    all_gather x1, blocking collectives, on_device(): lax.all_gather(valence, 'row', axis=0, tiled=True)  13.9 us
    all_gather x1, blocking collectives, on_device(): lax.all_gather(k_coords, 'row', axis=0, tiled=True)  13.5 us
    all_gather x1, blocking collectives, on_device(): lax.all_gather(vectors, 'row', axis=0, tiled=True)  12.8 us
    dot_general x8, matrix products, square_sweep(): jnp.einsum('ijg,jng->ing', coupling, col_proj, precision=highest)  8.74 us
  transfers between devices with their start and end apart: 3, of which 2 were waited for; matrix products, arithmetic and copies ran while one was open for 14% of the time, Pallas kernels for 0%

profile of v1, /device:TPU:0, one launch (start us, length us, event | category | flops | bytes accessed | tf_op | source)
XLA Modules:
  0.0 240.8 jit_solution(13974464845383612156)
XLA Ops:
  8.0 0.8 reshape.58
  8.8 1.7 convolution_bitcast_fusion.2
  11.2 13.5 %all-gather.2 = s32[8,2,2]{2,1,0:T(2,128)S(1)} all-gather(s32[1,2,2]{2,1,0:T(2,128)S(1)} %bitcast.65), channel_id=1, replica_groups=mesh['row'=8,'col'=4] {'row'}, dimensions={0}, use_global_device_ids=true | all-gather | bytes 144 | tf_op jit(solution)/shard_map/all_gather | solution.py:46
  24.7 8.1 %all-gather.1 = s32[4,2,2]{2,1,0:T(2,128)S(1)} all-gather(s32[1,2,2]{2,1,0:T(2,128)S(1)} %bitcast.66), channel_id=1, replica_groups=mesh['row'=8,'col'=4] {'col'}, dimensions={0}, use_global_device_ids=true | all-gather | bytes 80 | tf_op jit(solution)/shard_map/all_gather | solution.py:51
  32.8 13.9 %all_gather.23 = bf16[16,4,1024]{2,1,0:T(4,128)(2,1)S(1)} all-gather(bf16[2,4,1024]{2,1,0:T(4,128)(2,1)S(1)} %copy-done.2), channel_id=1, replica_groups=mesh['row'=8,'col'=4] {'row'}, dimensions={0}, use_global_device_ids=true | all-gather | bytes 147456 | tf_op jit(solution)/shard_map/all_gather | solution.py:44
  46.7 8.3 %all_gather.21 = bf16[8,4,1024]{2,1,0:T(4,128)(2,1)S(1)} all-gather(bf16[2,4,1024]{2,1,0:T(4,128)(2,1)S(1)} %copy-done.2), channel_id=1, replica_groups=mesh['row'=8,'col'=4] {'col'}, dimensions={0}, use_global_device_ids=true | all-gather | bytes 81920 | tf_op jit(solution)/shard_map/all_gather | solution.py:50
  55.1 14.0 %all_gather.24 = bf16[16,4,1024]{2,1,0:T(4,128)(2,1)S(1)} all-gather(bf16[2,4,1024]{2,1,0:T(4,128)(2,1)S(1)} %copy-done.3), channel_id=1, replica_groups=mesh['row'=8,'col'=4] {'row'}, dimensions={0}, use_global_device_ids=true | all-gather | bytes 147456 | tf_op jit(solution)/shard_map/all_gather | solution.py:43
  69.0 7.3 %all_gather.22 = bf16[8,4,1024]{2,1,0:T(4,128)(2,1)S(1)} all-gather(bf16[2,4,1024]{2,1,0:T(4,128)(2,1)S(1)} %copy-done.3), channel_id=1, replica_groups=mesh['row'=8,'col'=4] {'col'}, dimensions={0}, use_global_device_ids=true | all-gather | bytes 81920 | tf_op jit(solution)/shard_map/all_gather | solution.py:49
  78.1 12.8 %all-gather = bf16[8,2,512]{2,1,0:T(2,128)(2,1)S(1)} all-gather(bf16[1,2,512]{2,1,0:T(2,128)(2,1)S(1)} %bitcast.64), channel_id=1, replica_groups=mesh['row'=8,'col'=4] {'row'}, dimensions={0}, use_global_device_ids=true | all-gather | bytes 18432 | tf_op jit(solution)/shard_map/all_gather | solution.py:45
  90.9 33.2 %while.14 = (s32[]{:T(128)}, f32[8,16,32]{2,1,0:T(8,128)S(1)}, bf16[8,16,1024]{2,1,0:T(8,128)(2,1)S(1)}, bf16[16,16,1024]{2,1,0:T(8,128)(2,1)S(1)}, bf16[16,16,3...) while((s32[]{:T(128)}, f32[8,16,32]{2,1,0:T(8,128)S(1)}, ...), condition=%wide.region_3.4_spmd.clone, body=%wide.region_2.3_spmd.clone.sunk | while | flops 14714503 | bytes 2319689 | solution.py:73
  91.0 0.7 constant_dynamic-slice_fusion.2
  93.6 1.1 convolution_bitcast_fusion.8
  95.1 0.7 constant_dynamic-slice_fusion.2
  97.8 1.1 convolution_bitcast_fusion.8
  99.3 0.7 constant_dynamic-slice_fusion.2
  101.9 1.1 convolution_bitcast_fusion.8
  103.4 0.7 constant_dynamic-slice_fusion.2
  106.1 1.1 convolution_bitcast_fusion.8
  107.6 0.7 constant_dynamic-slice_fusion.2
  110.2 1.1 convolution_bitcast_fusion.8
  111.7 0.7 constant_dynamic-slice_fusion.2
  114.4 1.1 convolution_bitcast_fusion.8
  115.9 0.7 constant_dynamic-slice_fusion.2
  118.5 1.1 convolution_bitcast_fusion.8
  120.0 0.7 constant_dynamic-slice_fusion.2
  122.7 1.1 convolution_bitcast_fusion.8
  125.4 21.2 %reduce-scatter.4.cloned.1.call-done = f32[1,2,16,32]{3,2,1,0:T(8,128)} async-done(((f32[4,2,16,32]{3,2,1,0:T(8,128)}), f32[1,2,16,32]{3,2,1,0:T(8,128)}) %reduce-scatter.4.cloned.1.call-update) | async-done | bytes 4112
  146.6 44.5 %all-reduce.6.cloned.1.call-done = f32[1024,32]{0,1:T(8,128)} async-done(((f32[1024,32]{0,1:T(8,128)}), f32[1024,32]{0,1:T(8,128)}) %all-reduce.6.cloned.1.call-update) | async-done | bytes 131088 | tf_op jit(solution)/shard_map/psum | solution.py:39
  191.2 1.1 fusion.17
  192.5 39.3 %psum.23 = f32[32,32]{0,1:T(8,128)S(1)} all-reduce(f32[32,32]{0,1:T(8,128)S(1)} %convolution_bitcast_fusion.4), channel_id=1, replica_groups=mesh['row'=8,'col'=4] {'row','col'}, use_global_device_ids=true, to_apply=%region_5.6 | all-reduce | flops 1024 | bytes 8192 | tf_op jit(solution)/shard_map/psum | solution.py:95
  232.0 0.7 reshape.61
  232.7 0.7 copy.24
  (114 shorter events, 22.2 us)
Async XLA Ops:
  8.0 116.9 %all-reduce.4.cloned.1.call-start = ((), (), s32[]{:S(2)}) async-start(), calls=%async_computation.1 | async-start | bytes 262144 | tf_op jit(solution)/shard_map/psum | solution.py:39
  10.5 22.3 %copy-start.2 = (bf16[2,4,1024]{2,1,0:T(4,128)(2,1)S(1)}, bf16[2,4,1024]{2,1,0:T(4,128)(2,1)}, u32[]{:S(2)}) copy-start(bf16[2,4,1024]{2,1,0:T(4,128)(2,1)} %param.12) | copy-start | bytes 49156
  10.5 0.7 copy-start.6
  10.6 136.1 %reduce-scatter.4.cloned.1.call-start = ((), (), s32[]{:S(2)}) async-start(), calls=%async_computation.3 | async-start | bytes 81920
  46.7 8.3 %copy-start.3 = (bf16[2,4,1024]{2,1,0:T(4,128)(2,1)S(1)}, bf16[2,4,1024]{2,1,0:T(4,128)(2,1)}, u32[]{:S(2)}) copy-start(bf16[2,4,1024]{2,1,0:T(4,128)(2,1)} %param.11) | copy-start | bytes 49156
  77.4 0.7 copy-start.4
  124.2 0.6 copy-start
  124.8 66.3 %all-reduce.6.cloned.1.call-start = ((), (), s32[]{:S(2)}) async-start(), calls=%async_computation.2 | async-start | bytes 262144 | tf_op jit(solution)/shard_map/psum | solution.py:39
  124.9 66.2 %copy-start.1 = (bf16[2,16,1024]{2,1,0:T(8,128)(2,1)S(1)}, bf16[2,16,1024]{2,1,0:T(8,128)(2,1)}, u32[]{:S(2)}) copy-start(bf16[2,16,1024]{2,1,0:T(8,128)(2,1)} %param.10) | copy-start | bytes 196612
  124.9 66.2 %copy-start.5 = (f32[1024]{0:T(1024)S(1)}, f32[1024]{0:T(1024)}, u32[]{:S(2)}) copy-start(f32[1024]{0:T(1024)} %param.13) | copy-start | bytes 12292
  124.9 66.2 %copy-start.7 = (f32[2,16]{1,0:T(2,128)S(1)}, f32[2,16]{1,0:T(2,128)}, u32[]{:S(2)}) copy-start(f32[2,16]{1,0:T(2,128)} %param.15) | copy-start | bytes 388
Sparse Core Ops, SparseCore 0:
  11.1 57.6 all-reduce.3
Sparse Core Ops, SparseCore 1:
  124.9 21.7 reduce-scatter.3
  149.4 41.7 all-reduce.5
